TPU v7x, 32 devices: a whole 2x2x4 slice. The times are simulated.
32 devices in a mesh: tok: 8 (over y, x, core), exp: 4 (over z).
Axes of the slice: x: 2, y: 2, z: 4, core: 2. Of those that a mesh axis runs over, the one named last changes fastest.
Arguments:
- expert_rows: bfloat16 [4, 2048, 4096], P('exp', 'tok'), may hold values from -480 to 480
- router_input: bfloat16 [2048, 4096], P(('tok', 'exp')), may hold values from -6 to 6
- router_weight: float32 [4096, 4], replicated, may hold values from -0.09375 to 0.09375
- assign: int32 [2048, 2], P(('tok', 'exp')), may hold values from 0 to 3, all different within a row
- targets: int32 [2048], P(('tok', 'exp')), may hold values from 0 to 15999
- head: bfloat16 [4096, 16000], P('tok', 'exp'), may hold values from -0.35 to 0.35
Outputs:
- token_loss: float32 [2048], P(('tok', 'exp'))
- router_grad: float32 [4096, 4], replicated
- mean_loss: float32 [], replicated
All inputs are finite; a program needn't handle non-finite values.
Results may differ from a plain program's by a relative error of at most 0.007.
Values may be sent and summed in bfloat16 or wider, within the bound.
A program may use at most 128 MiB of HBM per device.

v0:
```python
import math
import jax
import jax.numpy as jnp
from jax import lax
from jax.sharding import PartitionSpec as P


def shards(expert_rows, router_input, router_weight, assign, targets, head):
    experts = router_weight.shape[1]
    own_rows = router_input.shape[0]
    tokens_all = own_rows * lax.axis_size("tok") * lax.axis_size("exp")
    loss_scale = 1.0 / math.sqrt(tokens_all)
    inputs = router_input.astype(jnp.float32)
    gate_logits = jnp.dot(inputs, router_weight, precision=lax.Precision.HIGHEST)
    labels = jnp.arange(experts, dtype=jnp.int32)
    first_hot = (assign[:, 0:1] == labels[None, :]).astype(jnp.float32)
    second_hot = (assign[:, 1:2] == labels[None, :]).astype(jnp.float32)
    differ = first_hot - second_hot
    mix_share = jax.nn.sigmoid(jnp.sum(gate_logits * differ, axis=1))
    mixing = mix_share[:, None] * first_hot + (1.0 - mix_share)[:, None] * second_hot
    local_rows = lax.all_to_all(expert_rows, "exp", split_axis=1, concat_axis=0, tiled=True)
    local_wide = local_rows.astype(jnp.float32)
    mixed_own = jnp.sum(mixing.T[:, :, None] * local_wide, axis=0).astype(jnp.bfloat16)
    mixed_rows, group_targets = (
        lax.all_gather(mixed_own, "exp", axis=0, tiled=True),
        lax.all_gather(targets, "exp", axis=0, tiled=True),
    )
    shard_width = head.shape[1]
    full_head = lax.all_gather(head, "tok", axis=0, tiled=True)
    logits = jnp.dot(mixed_rows, full_head, preferred_element_type=jnp.float32)
    first_col = lax.axis_index("exp") * shard_width
    columns = first_col + jnp.arange(shard_width, dtype=jnp.int32)
    target_hit = group_targets[:, None] == columns[None, :]
    picked = jnp.sum(jnp.where(target_hit, logits, 0.0), axis=1)
    local_top = jnp.max(logits, axis=1)
    row_top = lax.pmax(local_top, "exp")
    exp_total, target_logit = lax.psum(
        (jnp.sum(jnp.exp(logits - row_top[:, None]), axis=1), picked), "exp"
    )
    log_total = row_top + jnp.log(exp_total)
    group_loss = log_total - target_logit
    own_loss = lax.dynamic_slice_in_dim(group_loss, lax.axis_index("exp") * own_rows, own_rows, 0)
    loss_sum = lax.psum(jnp.sum(own_loss), ("tok", "exp"))
    slope = (
        loss_scale * (jnp.exp(logits - log_total[:, None]) - target_hit.astype(jnp.float32))
    ).astype(jnp.bfloat16)
    hidden_slope = lax.psum_scatter(
        lax.dot_general(
            slope, full_head, (((1,), (1,)), ((), ())), preferred_element_type=jnp.float32
        ).astype(jnp.bfloat16),
        "exp",
        scatter_dimension=0,
        tiled=True,
    ).astype(jnp.float32)
    weight_slope = jnp.sum(hidden_slope[None, :, :] * local_wide, axis=2).T
    spread = jnp.sum(weight_slope * differ, axis=1) * mix_share * (1.0 - mix_share)
    gate_slope = spread[:, None] * differ
    router_part = jnp.dot(inputs.T, gate_slope, precision=lax.Precision.HIGHEST)
    router_sum = lax.psum(router_part, ("tok", "exp"))
    mean_loss = loss_sum / tokens_all
    return (own_loss, router_sum, mean_loss)


def solution(mesh):
    in_specs = (
        P("exp", "tok", None),
        P(("tok", "exp"), None),
        P(),
        P(("tok", "exp"), None),
        P(("tok", "exp")),
        P("tok", "exp"),
    )
    out_specs = (P(("tok", "exp")), P(), P())
    return jax.shard_map(shards, mesh=mesh, in_specs=in_specs, out_specs=out_specs, check_vma=False)
```

profile of v0, /device:TPU:1, one launch (start us, length us, event | category | flops | bytes accessed | tf_op | source)
XLA Modules:
  0.0 542.0 jit_solution(5459968139769704115)
XLA Ops:
  7.2 0.0 copy-start
  7.2 8.4 %copy.16 = bf16[1,256,4096]{2,0,1:T(2,128)(2,1)} copy(bf16[1,256,4096]{2,1,0:T(8,128)(2,1)} %param.6) | data formatting | bytes 4194304 | tf_op args[0]
  15.6 0.5 broadcast.107
  16.1 13.5 %reduce.1 = bf16[256,4096]{1,0:T(8,128)(2,1)S(1)} reduce(bf16[256,1,4096]{2,1,0:T(2,128)(2,1)} %bitcast.29, bf16[]{:T(256)} %broadcast.107), dimensions={1}, to_apply=%bitcast.25.reduce_sub_computation | reduce | bytes 4194306
  29.6 0.0 copy-start.3
  29.6 0.0 copy-start.2
  29.6 2.8 reshape.110
  32.4 5.4 all-to-all-start
  37.8 0.0 all-gather.3.cloned.1.call-start
  37.8 0.0 copy-done.3
  37.8 0.0 copy-done
  37.8 0.0 copy-done.2
  37.9 0.5 fusion.10
  38.4 47.2 %all-to-all-done = bf16[4,2,131072]{2,1,0:T(2,128)(2,1)S(1)} async-done(((bf16[4,2,131072]{2,1,0:T(2,128)(2,1)}), bf16[4,2,131072]{2,1,0:T(2,128)(2,1)S(1)}, u32[]{:S(2)}, u32[]{:S(2)}) %all-to-all-start) | async-done | bytes 2097184 | tf_op jit(solution)/shard_map/all_to_all | solution.py:21
  85.6 3.3 reshape.111
  88.9 6.0 %copy_convert_fusion = f32[1,256,4096]{2,1,0:T(8,128)S(1)} fusion(bf16[1,256,4096]{2,0,1:T(2,128)(2,1)} %bitcast.27), kind=kLoop, calls=%fused_computation.12 | loop fusion | flops 1048576 | bytes 6291456 | tf_op jit(solution)/shard_map/convert_element_type | solution.py:22
  94.9 0.0 copy-start.5
  94.9 0.0 copy-start.4
  94.9 1.4 multiply_reduce_fusion
  96.3 0.0 all-gather.3.cloned.1.call-update
  96.3 0.0 all-gather.5.cloned.1.call-start
  96.3 0.7 all-gather.5.cloned.1.call-update
  97.1 0.2 reduce-scatter.2.cloned.1.call-start
  97.3 0.0 copy-done.5
  97.3 0.6 dynamic-slice
  98.5 0.0 copy-done.4
  98.6 0.2 dynamic-update-slice
  98.8 4.0 all-reduce
  102.8 39.0 %all-gather.3.cloned.1.call-done = bf16[256,4096]{1,0:T(8,128)(2,1)} async-done(((bf16[64,4096]{1,0:T(8,128)(2,1)}), bf16[256,4096]{1,0:T(8,128)(2,1)}) %all-gather.3.cloned.1.call-update) | async-done | bytes 2097168 | tf_op jit(solution)/shard_map/all_gather | solution.py:25
  141.8 165.1 %all-gather.5.cloned.1.call-done = bf16[4096,4000]{0,1:T(8,128)(2,1)} async-done(((bf16[512,4000]{0,1:T(8,128)(2,1)}), bf16[4096,4000]{0,1:T(8,128)(2,1)}) %all-gather.5.cloned.1.call-update) | async-done | bytes 32768016 | tf_op jit(solution)/shard_map/all_gather | solution.py:29
  306.9 16.2 %fusion.19 = (f32[256]{0:T(256)S(1)}, f32[256,4000]{0,1:T(8,128)}) fusion(bf16[256,4096]{1,0:T(8,128)(2,1)} %all-gather.3.cloned.1.call-done, bf16[4096,4000]{0,1:T(8,128)(2,1)} %all-gather.5.cloned.1.call-done), kind=kOutput, calls=%fused_computation.41 | convolution fusion | flops 8389632000 | bytes 38962176 | tf_op jit(solution)/shard_map/dot_general | solution.py:30
  323.2 9.7 %pmax.7 = f32[256]{0:T(256)S(1)} all-reduce(f32[256]{0:T(256)S(1)} %get-tuple-element.15), channel_id=1, replica_groups=mesh['tok'=8,'exp'=4] {'exp'}, use_global_device_ids=true, to_apply=%region_3.4 | all-reduce | flops 256 | bytes 2048 | tf_op jit(solution)/shard_map/pmax | solution.py:36
  332.8 3.9 fusion.1
  336.7 6.6 %all-reduce.1 = (f32[256]{0:T(256)S(1)}, f32[256]{0:T(256)S(1)}) all-reduce(f32[256]{0:T(256)S(1)} %get-tuple-element.4, f32[256]{0:T(256)S(1)} %get-tuple-element.3), channel_id=1, replica_groups=mesh['tok'=8,'exp'=4] {'exp'}, use_global_device_ids=true, to_apply=%region_5.6 | all-reduce | flops 512 | bytes 4096 | tf_op jit(solution)/shard_map/psum | solution.py:37
  343.3 17.2 %convolution_convert_fusion = bf16[256,4096]{1,0:T(8,128)(2,1)} fusion(bf16[4096,4000]{0,1:T(8,128)(2,1)} %all-gather.5.cloned.1.call-done, f32[256,4000]{0,1:T(8,128)} %get-tuple-element.16, f32[256]{0:T(256)S(1)} %get-tuple-element.10, s32[256]{0:T(256)S(1)} %all-reduce, s32[4000]{0:T(1024)S(1)} %iota_add_fusion), kind=kOutput, calls=%fused_computation | convolution fusion | flops 8395800576 | bytes 38979200 | tf_op jit(solution)/shard_map/dot_general | solution.py:48
  360.5 0.0 reduce-scatter.2.cloned.1.call-update
  360.5 0.0 all-reduce.4.cloned.1.call-start
  360.6 45.4 %reduce-scatter.2.cloned.1.call-done = bf16[64,4096]{1,0:T(8,128)(2,1)} async-done(((bf16[256,4096]{1,0:T(8,128)(2,1)}), bf16[64,4096]{1,0:T(8,128)(2,1)}) %reduce-scatter.2.cloned.1.call-update) | async-done | bytes 524304 | tf_op jit(solution)/shard_map/reduce_scatter | solution.py:47
  406.0 0.0 copy-start.1
  406.0 1.7 mul.89
  407.6 0.7 copy-done.1
  408.3 2.4 fusion
  410.7 0.1 reduce_sum.70
  410.8 1.0 convolution_bitcast_fusion
  411.8 0.0 all-reduce.4.cloned.1.call-update
  411.8 1.2 fusion.17
  413.0 39.8 %psum.31 = f32[]{:T(128)} all-reduce(f32[]{:T(128)} %get-tuple-element.7), channel_id=1, replica_groups=mesh['tok'=8,'exp'=4] {'tok','exp'}, use_global_device_ids=true, to_apply=%region_13.14 | all-reduce | flops 1 | bytes 8 | tf_op jit(solution)/shard_map/psum | solution.py:43
  453.4 79.5 %all-reduce.4.cloned.1.call-done = f32[4096,4]{0,1:T(4,128)} async-done(((f32[4096,4]{0,1:T(4,128)}), f32[4096,4]{0,1:T(4,128)}) %all-reduce.4.cloned.1.call-update) | async-done | bytes 65552 | tf_op jit(solution)/shard_map/psum | solution.py:59
  532.9 1.5 copy.19
  (8 shorter events, 0.1 us)
Async XLA Ops:
  7.2 30.7 %copy-start = (bf16[64,4096]{1,0:T(8,128)(2,1)S(1)}, bf16[64,4096]{1,0:T(8,128)(2,1)}, u32[]{:S(2)}) copy-start(bf16[64,4096]{1,0:T(8,128)(2,1)} %param.7) | copy-start | bytes 1572868
  29.6 8.2 %copy-start.3 = (s32[64,2]{0,1:T(2,128)S(1)}, s32[64,2]{0,1:T(2,128)}, u32[]{:S(2)}) copy-start(s32[64,2]{0,1:T(2,128)} %param.9) | copy-start | bytes 1540
  29.6 8.2 %copy-start.2 = (f32[4096,4]{0,1:T(4,128)S(1)}, f32[4096,4]{0,1:T(4,128)}, u32[]{:S(2)}) copy-start(f32[4096,4]{0,1:T(4,128)} %param.8) | copy-start | bytes 196612
  32.4 53.2 %all-to-all-start = ((bf16[4,2,131072]{2,1,0:T(2,128)(2,1)}), bf16[4,2,131072]{2,1,0:T(2,128)(2,1)S(1)}, u32[]{:S(2)}, u32[]{:S(2)}) async-start(bf16[4,2,131072]{2,1,0:T(2,128)(2,1)} %reshape.110), calls=%async_computation | async-start | bytes 4194304 | tf_op jit(solution)/shard_map/all_to_all | solution.py:21
  37.8 104.0 %all-gather.3.cloned.1.call-start = ((), (), s32[]{:S(2)}) async-start(), calls=%async_computation.2 | async-start | bytes 2621440 | tf_op jit(solution)/shard_map/all_gather | solution.py:25
  94.9 2.4 copy-start.5
  94.9 3.6 copy-start.4
  96.3 210.6 %all-gather.5.cloned.1.call-start = ((), (), s32[]{:S(2)}) async-start(), calls=%async_computation.3 | async-start | bytes 36864000 | tf_op jit(solution)/shard_map/all_gather | solution.py:29
  97.1 308.9 %reduce-scatter.2.cloned.1.call-start = ((), (), s32[]{:S(2)}) async-start(), calls=%async_computation.4 | async-start | bytes 2621440 | tf_op jit(solution)/shard_map/reduce_scatter | solution.py:47
  360.5 172.3 %all-reduce.4.cloned.1.call-start = ((), (), s32[]{:S(2)}) async-start(), calls=%async_computation.5 | async-start | bytes 131072 | tf_op jit(solution)/shard_map/psum | solution.py:59
  406.0 2.3 copy-start.1
Sparse Core Ops, SparseCore 0:
  96.4 45.3 all-gather.2
  143.6 163.2 all-gather.4
  360.7 45.2 reduce-scatter.1
  412.0 120.8 all-reduce.3
where the time goes:
time: 543 us; the launch traced here: 542 us
  waiting for transfers between devices  377 us (69%)
  blocking collectives  60.1 us (11%)
  matrix products  34.9 us (6%)
  other arithmetic  28.4 us (5%)
  local copies, waits for them, and re-layouts  19.7 us (4%)
  between operations  16.3 us (3%)
  starting transfers between devices  5.71 us (1%)
    all_gather x1, waiting for transfers between devices, shards(): full_head = lax.all_gather(head, 'tok', axis=0, tiled=True)  165 us
    psum x1, waiting for transfers between devices, shards(): router_sum = lax.psum(router_part, ('tok', 'exp'))  79.5 us
    all_to_all x1, waiting for transfers between devices, shards(): lax.all_to_all(expert_rows, 'exp', split_axis=1, concat_axis=0, tiled=True)  47.2 us
    reduce_scatter x1, waiting for transfers between devices, shards(): lax.psum_scatter(lax.dot_general(slope, full_head, (((1,), (1,)), ((), ()...  45.4 us
    psum x1, blocking collectives, shards(): loss_sum = lax.psum(jnp.sum(own_loss), ('tok', 'exp'))  39.8 us
    all_gather x1, waiting for transfers between devices, shards(): lax.all_gather(mixed_own, 'exp', axis=0, tiled=True)  39 us
    unnamed x20, local copies, waits for them, and re-layouts  18 us
    dot_general x1, matrix products, shards(): lax.dot_general(slope, full_head, (((1,), (1,)), ((), ())), preferred_ele...  17.2 us
  transfers between devices with their start and end apart: 5, of which 5 were waited for; matrix products, arithmetic and copies ran while one was open for 0% of the time, Pallas kernels for 0%

commit v1 on v0

--- a/solution.py
+++ b/solution.py
@@ -56,7 +56,7 @@
     spread = jnp.sum(weight_slope * differ, axis=1) * mix_share * (1.0 - mix_share)
     gate_slope = spread[:, None] * differ
     router_part = jnp.dot(inputs.T, gate_slope, precision=lax.Precision.HIGHEST)
-    router_sum = lax.psum(router_part, ("tok", "exp"))
+    router_sum = jnp.sum(lax.all_gather(router_part, ("tok", "exp")), axis=0)
     mean_loss = loss_sum / tokens_all
     return (own_loss, router_sum, mean_loss)
 

time: 543 us -> 480 us (0.88)
  waiting for transfers between devices: 377 us -> 313 us
    psum x1 -> x0, waiting for transfers between devices: 79.5 us -> none  [shards(): router_sum = lax.psum(router_part, ('tok', 'exp'))]
    all_gather x0 -> x1, waiting for transfers between devices: none -> 15.3 us  [shards(): router_sum = jnp.sum(lax.all_gather(router_part, ('tok', 'exp')), axis=0)]
    unnamed x20 -> x19, local copies, waits for them, and re-layouts: 18 us -> 16.5 us
  transfers between devices with their start and end apart: 5 -> 5, of which waited for: 5 -> 5; matrix products, arithmetic and copies ran while one was open for 0% -> 1% of each run, Pallas kernels for 0% -> 0%
where the time goes in v1:
time: 480 us
  waiting for transfers between devices  313 us (65%)
  blocking collectives  59.8 us (12%)
  matrix products  34.9 us (7%)
  other arithmetic  31.9 us (7%)
  local copies, waits for them, and re-layouts  18.3 us (4%)
  between operations  16.3 us (3%)
  starting transfers between devices  5.71 us (1%)
    all_gather x1, waiting for transfers between devices, shards(): full_head = lax.all_gather(head, 'tok', axis=0, tiled=True)  165 us
    all_to_all x1, waiting for transfers between devices, shards(): lax.all_to_all(expert_rows, 'exp', split_axis=1, concat_axis=0, tiled=True)  47.2 us
    reduce_scatter x1, waiting for transfers between devices, shards(): lax.psum_scatter(lax.dot_general(slope, full_head, (((1,), (1,)), ((), ()...  45.4 us
    psum x1, blocking collectives, shards(): loss_sum = lax.psum(jnp.sum(own_loss), ('tok', 'exp'))  39.5 us
    all_gather x1, waiting for transfers between devices, shards(): lax.all_gather(mixed_own, 'exp', axis=0, tiled=True)  39 us
    dot_general x1, matrix products, shards(): lax.dot_general(slope, full_head, (((1,), (1,)), ((), ())), preferred_ele...  17.2 us
    unnamed x19, local copies, waits for them, and re-layouts  16.5 us
    dot_general x1, matrix products, shards(): logits = jnp.dot(mixed_rows, full_head, preferred_element_type=jnp.float32)  16.2 us
  transfers between devices with their start and end apart: 5, of which 5 were waited for; matrix products, arithmetic and copies ran while one was open for 1% of the time, Pallas kernels for 0%

profile of v1, /device:TPU:1, one launch (start us, length us, event | category | flops | bytes accessed | tf_op | source)
XLA Modules:
  0.0 479.5 jit_solution(8469305248680894103)
XLA Ops:
  7.2 0.0 copy-start
  7.2 8.4 %copy.18 = bf16[1,256,4096]{2,0,1:T(2,128)(2,1)} copy(bf16[1,256,4096]{2,1,0:T(8,128)(2,1)} %param.6) | data formatting | bytes 4194304 | tf_op args[0]
  15.6 0.5 broadcast.107
  16.1 13.5 %reduce.1 = bf16[256,4096]{1,0:T(8,128)(2,1)S(1)} reduce(bf16[256,1,4096]{2,1,0:T(2,128)(2,1)} %bitcast.34, bf16[]{:T(256)} %broadcast.107), dimensions={1}, to_apply=%bitcast.30.reduce_sub_computation | reduce | bytes 4194306
  29.6 0.0 copy-start.3
  29.6 0.0 copy-start.2
  29.6 2.8 reshape.111
  32.4 5.4 %all-to-all-start = ((bf16[4,2,131072]{2,1,0:T(2,128)(2,1)}), bf16[4,2,131072]{2,1,0:T(2,128)(2,1)S(1)}, u32[]{:S(2)}, u32[]{:S(2)}) async-start(bf16[4,2,131072]{2,1,0:T(2,128)(2,1)} %reshape.111), calls=%async_computation | async-start | bytes 4194304 | tf_op jit(solution)/shard_map/all_to_all | solution.py:21
  37.8 0.0 all-gather.5.cloned.1.call-start
  37.8 0.0 copy-done.3
  37.8 0.0 copy-done
  37.8 0.0 copy-done.2
  37.9 0.5 fusion.10
  38.4 47.2 %all-to-all-done = bf16[4,2,131072]{2,1,0:T(2,128)(2,1)S(1)} async-done(((bf16[4,2,131072]{2,1,0:T(2,128)(2,1)}), bf16[4,2,131072]{2,1,0:T(2,128)(2,1)S(1)}, u32[]{:S(2)}, u32[]{:S(2)}) %all-to-all-start) | async-done | bytes 2097184 | tf_op jit(solution)/shard_map/all_to_all | solution.py:21
  85.6 3.3 reshape.112
  88.9 6.0 %copy_convert_fusion = f32[1,256,4096]{2,1,0:T(8,128)S(1)} fusion(bf16[1,256,4096]{2,0,1:T(2,128)(2,1)} %bitcast.32), kind=kLoop, calls=%fused_computation.13 | loop fusion | flops 1048576 | bytes 6291456 | tf_op jit(solution)/shard_map/convert_element_type | solution.py:22
  94.9 0.0 copy-start.5
  94.9 0.0 copy-start.4
  94.9 1.4 multiply_reduce_fusion
  96.3 0.0 all-gather.5.cloned.1.call-update
  96.3 0.0 all-gather.7.cloned.1.call-start
  96.3 0.7 all-gather.7.cloned.1.call-update
  97.1 0.2 reduce-scatter.2.cloned.1.call-start
  97.3 0.0 copy-done.5
  97.3 0.6 dynamic-slice
  98.5 0.0 copy-done.4
  98.6 0.2 dynamic-update-slice
  98.8 4.0 all-reduce
  102.8 39.0 %all-gather.5.cloned.1.call-done = bf16[256,4096]{1,0:T(8,128)(2,1)} async-done(((bf16[64,4096]{1,0:T(8,128)(2,1)}), bf16[256,4096]{1,0:T(8,128)(2,1)}) %all-gather.5.cloned.1.call-update) | async-done | bytes 2097168 | tf_op jit(solution)/shard_map/all_gather | solution.py:25
  141.8 165.1 %all-gather.7.cloned.1.call-done = bf16[4096,4000]{0,1:T(8,128)(2,1)} async-done(((bf16[512,4000]{0,1:T(8,128)(2,1)}), bf16[4096,4000]{0,1:T(8,128)(2,1)}) %all-gather.7.cloned.1.call-update) | async-done | bytes 32768016 | tf_op jit(solution)/shard_map/all_gather | solution.py:29
  306.9 16.2 %fusion.19 = (f32[256]{0:T(256)S(1)}, f32[256,4000]{0,1:T(8,128)}) fusion(bf16[256,4096]{1,0:T(8,128)(2,1)} %all-gather.5.cloned.1.call-done, bf16[4096,4000]{0,1:T(8,128)(2,1)} %all-gather.7.cloned.1.call-done), kind=kOutput, calls=%fused_computation.42 | convolution fusion | flops 8389632000 | bytes 38962176 | tf_op jit(solution)/shard_map/dot_general | solution.py:30
  323.2 9.7 %pmax.7 = f32[256]{0:T(256)S(1)} all-reduce(f32[256]{0:T(256)S(1)} %get-tuple-element.15), channel_id=1, replica_groups=mesh['tok'=8,'exp'=4] {'exp'}, use_global_device_ids=true, to_apply=%region_3.4 | all-reduce | flops 256 | bytes 2048 | tf_op jit(solution)/shard_map/pmax | solution.py:36
  332.8 3.9 fusion.1
  336.7 6.6 %all-reduce.1 = (f32[256]{0:T(256)S(1)}, f32[256]{0:T(256)S(1)}) all-reduce(f32[256]{0:T(256)S(1)} %get-tuple-element.4, f32[256]{0:T(256)S(1)} %get-tuple-element.3), channel_id=1, replica_groups=mesh['tok'=8,'exp'=4] {'exp'}, use_global_device_ids=true, to_apply=%region_5.6 | all-reduce | flops 512 | bytes 4096 | tf_op jit(solution)/shard_map/psum | solution.py:37
  343.3 17.2 %convolution_convert_fusion = bf16[256,4096]{1,0:T(8,128)(2,1)} fusion(bf16[4096,4000]{0,1:T(8,128)(2,1)} %all-gather.7.cloned.1.call-done, f32[256,4000]{0,1:T(8,128)} %get-tuple-element.16, f32[256]{0:T(256)S(1)} %get-tuple-element.10, s32[256]{0:T(256)S(1)} %all-reduce, s32[4000]{0:T(1024)S(1)} %iota_add_fusion), kind=kOutput, calls=%fused_computation | convolution fusion | flops 8395800576 | bytes 38979200 | tf_op jit(solution)/shard_map/dot_general | solution.py:48
  360.5 0.0 reduce-scatter.2.cloned.1.call-update
  360.5 0.0 all-gather.9.cloned.1.call-start
  360.6 45.4 %reduce-scatter.2.cloned.1.call-done = bf16[64,4096]{1,0:T(8,128)(2,1)} async-done(((bf16[256,4096]{1,0:T(8,128)(2,1)}), bf16[64,4096]{1,0:T(8,128)(2,1)}) %reduce-scatter.2.cloned.1.call-update) | async-done | bytes 524304 | tf_op jit(solution)/shard_map/reduce_scatter | solution.py:47
  406.0 0.0 copy-start.1
  406.0 1.7 mul.89
  407.6 0.7 copy-done.1
  408.3 2.4 fusion
  410.7 0.1 reduce_sum.79
  410.8 1.0 convolution_bitcast_fusion
  411.8 0.0 all-gather.9.cloned.1.call-update
  411.8 1.2 fusion.17
  413.0 39.5 %psum.23 = f32[]{:T(128)} all-reduce(f32[]{:T(128)} %get-tuple-element.7), channel_id=1, replica_groups=mesh['tok'=8,'exp'=4] {'tok','exp'}, use_global_device_ids=true, to_apply=%region_13.14 | all-reduce | flops 1 | bytes 8 | tf_op jit(solution)/shard_map/psum | solution.py:43
  453.1 15.3 %all-gather.9.cloned.1.call-done = f32[131072,4]{0,1:T(4,128)} async-done(((f32[4096,4]{0,1:T(4,128)}), f32[131072,4]{0,1:T(4,128)}) %all-gather.9.cloned.1.call-update) | async-done | bytes 2097168 | tf_op jit(solution)/shard_map/all_gather | solution.py:59
  468.4 3.5 bitcast_reduce_fusion
  (8 shorter events, 0.1 us)
Async XLA Ops:
  7.2 30.7 %copy-start = (bf16[64,4096]{1,0:T(8,128)(2,1)S(1)}, bf16[64,4096]{1,0:T(8,128)(2,1)}, u32[]{:S(2)}) copy-start(bf16[64,4096]{1,0:T(8,128)(2,1)} %param.7) | copy-start | bytes 1572868
  29.6 8.2 %copy-start.3 = (s32[64,2]{0,1:T(2,128)S(1)}, s32[64,2]{0,1:T(2,128)}, u32[]{:S(2)}) copy-start(s32[64,2]{0,1:T(2,128)} %param.9) | copy-start | bytes 1540
  29.6 8.2 %copy-start.2 = (f32[4096,4]{0,1:T(4,128)S(1)}, f32[4096,4]{0,1:T(4,128)}, u32[]{:S(2)}) copy-start(f32[4096,4]{0,1:T(4,128)} %param.8) | copy-start | bytes 196612
  32.4 53.2 %all-to-all-start = ((bf16[4,2,131072]{2,1,0:T(2,128)(2,1)}), bf16[4,2,131072]{2,1,0:T(2,128)(2,1)S(1)}, u32[]{:S(2)}, u32[]{:S(2)}) async-start(bf16[4,2,131072]{2,1,0:T(2,128)(2,1)} %reshape.111), calls=%async_computation | async-start | bytes 4194304 | tf_op jit(solution)/shard_map/all_to_all | solution.py:21
  37.8 104.0 %all-gather.5.cloned.1.call-start = ((), (), s32[]{:S(2)}) async-start(), calls=%async_computation.2 | async-start | bytes 2621440 | tf_op jit(solution)/shard_map/all_gather | solution.py:25
  94.9 2.4 copy-start.5
  94.9 3.6 copy-start.4
  96.3 210.6 %all-gather.7.cloned.1.call-start = ((), (), s32[]{:S(2)}) async-start(), calls=%async_computation.3 | async-start | bytes 36864000 | tf_op jit(solution)/shard_map/all_gather | solution.py:29
  97.1 308.9 %reduce-scatter.2.cloned.1.call-start = ((), (), s32[]{:S(2)}) async-start(), calls=%async_computation.4 | async-start | bytes 2621440 | tf_op jit(solution)/shard_map/reduce_scatter | solution.py:47
  360.5 107.9 %all-gather.9.cloned.1.call-start = ((), (), s32[]{:S(2)}) async-start(), calls=%async_computation.5 | async-start | bytes 2162688 | tf_op jit(solution)/shard_map/all_gather | solution.py:59
  406.0 2.3 copy-start.1
Sparse Core Ops, SparseCore 0:
  96.4 45.3 all-gather.4
  143.6 163.2 all-gather.6
  360.7 45.2 reduce-scatter.1
  411.9 56.4 all-gather.8
